TPU v7x, 32 devices: a whole 2x2x4 slice. The times are simulated.
32 devices in a mesh: section: 4 (over x, core), row: 2 (over y), col: 4 (over z).
Axes of the slice: x: 2, y: 2, z: 4, core: 2. Of those that a mesh axis runs over, the one named last changes fastest.
Arguments:
- hidden: bfloat16 [4, 8, 4096], P(None, None, 'col'), may hold values from -6 to 6
- norm_gain: bfloat16 [4, 4096], P('section', 'col'), may hold values from 0.25 to 1.75
- w_qkv: bfloat16 [4, 4096, 6144], P('section', 'col', 'row'), may hold values from -0.09375 to 0.09375
- w_out: bfloat16 [4, 4096, 4096], P('section', 'row', 'col'), may hold values from -0.09375 to 0.09375
- cache_keys: bfloat16 [4, 4, 8, 128, 8, 128], P('section', None, 'col', None, 'row'), may hold values from -240 to 240, as said below
- cache_values: bfloat16 [4, 4, 8, 128, 8, 128], P('section', None, 'col', None, 'row'), may hold values from -6 to 6
- cache_lengths: int32 [4, 8], P(None, 'col'), may hold values from 1 to 127
Outputs:
- layer_outputs: bfloat16 [4, 4, 8, 4096], P('section', None, None, 'col')
Inputs may be any that keep to these rules, and one draw needn't show every extreme that they name: `cache_keys`: cached keys are of order one except that some sequences may carry much larger keys at a few positions.
All inputs are finite; a program needn't handle non-finite values.
Results may differ from a plain program's by a relative error of at most 0.04.
Values may be sent and summed in bfloat16 or wider, within the bound.
A program may use at most 64 MiB of HBM per device.

v0:
```python
import jax
import jax.numpy as jnp
from jax import lax
from jax.sharding import PartitionSpec as P

D = 4096
HEADS = 32
KVH = 8


def from_behind(x, axis, by):
    peers = lax.axis_size(axis)
    pairs = [(i, i + by) for i in range(peers) if 0 <= i + by < peers]
    return lax.ppermute(x, axis, pairs)


def rotate(vectors, positions):
    half_dim = vectors.shape[-1] // 2
    inverse_freq = 500000.0 ** (-jnp.arange(half_dim, dtype=jnp.float32) * 2.0 / vectors.shape[-1])
    angles = positions * inverse_freq
    angles = jnp.concatenate([angles, angles], axis=-1)
    swapped = jnp.concatenate([-vectors[..., half_dim:], vectors[..., :half_dim]], axis=-1)
    return vectors * jnp.cos(angles) + swapped * jnp.sin(angles)


def attend(queries, new_key, new_value, key_block, value_block, length):
    score_scale = 1.0 / jnp.sqrt(jnp.float32(queries.shape[-1]))
    scores = (
        jnp.einsum("bgrd,bjgd->bgrj", queries, key_block, preferred_element_type=jnp.float32)
        * score_scale
    )
    own_score = (
        jnp.einsum("bgrd,bgd->bgr", queries, new_key, preferred_element_type=jnp.float32)
        * score_scale
    )
    visible = jnp.arange(key_block.shape[1])[None, :] < length[:, None]
    scores = jnp.where(visible[:, None, None, :], scores, -jnp.inf)
    row_max = jnp.maximum(jnp.max(scores, axis=-1), own_score)
    cache_exp = jnp.exp(scores - row_max[..., None])
    own_exp = jnp.exp(own_score - row_max)
    total = jnp.sum(cache_exp, axis=-1) + own_exp
    cache_weight = (cache_exp / total[..., None]).astype(jnp.bfloat16)
    own_weight = (own_exp / total).astype(jnp.bfloat16)
    result = jnp.einsum(
        "bgrj,bjgd->bgrd", cache_weight, value_block, preferred_element_type=jnp.float32
    )
    result = (
        result
        + own_weight.astype(jnp.float32)[..., None] * new_value.astype(jnp.float32)[:, :, None, :]
    )
    return result.astype(jnp.bfloat16)


def shards(hidden, norm_gain, w_qkv, w_out, cache_keys, cache_values, cache_lengths):
    section_count = lax.axis_size("section")
    section_at = lax.axis_index("section")
    col_count = lax.axis_size("col")
    micro_count = hidden.shape[0]
    batch_size = hidden.shape[1]
    seq_part = batch_size // col_count
    gain_row = norm_gain[0]
    proj_weight = w_qkv[0]
    out_weight = w_out[0]
    groups = cache_keys.shape[4]
    head_dim = cache_keys.shape[5]
    per_group = HEADS // KVH
    tick_count = micro_count + section_count - 1

    def layer_part(current, key_block, value_block, length):
        h_float = current.astype(jnp.float32)
        scaled = (h_float * gain_row.astype(jnp.float32)).astype(jnp.bfloat16)
        squares = jnp.sum(h_float * h_float, axis=1)
        partial_value = jnp.dot(scaled, proj_weight, preferred_element_type=jnp.float32)
        projected, own_squares = (
            lax.psum_scatter(partial_value, "col", scatter_dimension=0, tiled=True),
            lax.psum_scatter(squares, "col", scatter_dimension=0, tiled=True),
        )
        factor = lax.rsqrt(own_squares / D + 1e-05)
        projected = (projected * factor[:, None]).reshape(seq_part, groups, per_group + 2, head_dim)
        positions = length.astype(jnp.float32)
        queries = rotate(projected[:, :, :per_group], positions[:, None, None, None]).astype(
            jnp.bfloat16
        )
        new_key = rotate(projected[:, :, per_group], positions[:, None, None]).astype(jnp.bfloat16)
        new_value = projected[:, :, per_group + 1].astype(jnp.bfloat16)
        attended = attend(queries, new_key, new_value, key_block, value_block, length)
        attended = attended.reshape(seq_part, groups * per_group * head_dim)
        mixed_rows = jnp.dot(
            lax.all_gather(attended, "col", axis=0, tiled=True),
            out_weight,
            preferred_element_type=jnp.float32,
        )
        summed = lax.psum(mixed_rows, "row")
        return (h_float + summed).astype(jnp.bfloat16)

    def advance(tick_at, loop_state):
        received, collected = loop_state
        micro_at = tick_at - section_at
        active = (micro_at >= 0) & (micro_at < micro_count)
        micro_pick = jnp.clip(micro_at, 0, micro_count - 1)
        entry_rows = lax.dynamic_index_in_dim(
            hidden, jnp.clip(tick_at, 0, micro_count - 1), 0, keepdims=False
        )
        current = jnp.where(section_at == 0, entry_rows, received)
        key_block = lax.dynamic_index_in_dim(cache_keys[0], micro_pick, 0, keepdims=False)
        value_block = lax.dynamic_index_in_dim(cache_values[0], micro_pick, 0, keepdims=False)
        length = lax.dynamic_index_in_dim(cache_lengths, micro_pick, 0, keepdims=False)
        produced = layer_part(current, key_block, value_block, length)
        previous = lax.dynamic_index_in_dim(collected, micro_pick, 0, keepdims=False)
        stored = jnp.where(active, produced, previous)
        collected = lax.dynamic_update_index_in_dim(collected, stored, micro_pick, 0)
        received = from_behind(produced, "section", 1)
        return (received, collected)

    start_rows = jnp.zeros(hidden.shape[1:], jnp.bfloat16)
    start_collected = jnp.zeros(hidden.shape, jnp.bfloat16)
    received, collected = lax.fori_loop(0, tick_count, advance, (start_rows, start_collected))
    return collected[None]


def solution(mesh):
    return jax.shard_map(
        shards,
        mesh=mesh,
        in_specs=(
            P(None, None, "col"),
            P("section", "col"),
            P("section", "col", "row"),
            P("section", "row", "col"),
            P("section", None, "col", None, "row", None),
            P("section", None, "col", None, "row", None),
            P(None, "col"),
        ),
        out_specs=P("section", None, None, "col"),
        check_vma=False,
    )
```

profile of v0, /device:TPU:1, one launch (start us, length us, event | category | flops | bytes accessed | tf_op | source)
XLA Modules:
  0.0 510.5 jit_solution(13046033242243475409)
XLA Ops:
  8.0 495.0 %while.18 = (s32[]{:T(128)}, bf16[8,1024]{1,0:T(8,128)(2,1)S(1)}, bf16[4,8,1024]{2,1,0:T(8,128)(2,1)S(1)}, pred[]{:T(512)}, bf16[4,8,1024]{2,1,0:T(8,128)(2,1)},...) while((s32[]{:T(128)}, bf16[8,1024]{1,0:T(8,128)(2,1)S(1)}, ...), condition=%wide.region_7.8_spmd, body=%wide.region_0.7_spmd.sunk | while | flops 86196720 | bytes 13568984 | solution.py:117
  9.0 4.3 fusion.65
  13.7 10.8 %all-reduce.5 = f32[8]{0:T(128)S(1)} all-reduce(f32[8]{0:T(128)S(1)} %get-tuple-element.477), channel_id=3, replica_groups=mesh['section'=4,'row'=2,'col'=4] {'col'}, use_global_device_ids=true, to_apply=%region_3.3.clone | all-reduce | flops 8 | bytes 64 | tf_op jit(solution)/shard_map/while
  25.6 1.2 constant_dynamic-slice_fusion.7
  26.9 21.0 %all-reduce.8.cloned.1.call-done = f32[8,3072]{1,0:T(8,128)} async-done(((f32[8,3072]{1,0:T(8,128)}), f32[8,3072]{1,0:T(8,128)}) %all-reduce.8.cloned.1.call-update) | async-done | bytes 98320 | tf_op jit(solution)/shard_map/while
  47.9 1.0 dynamic-slice_multiply_fusion.3
  50.2 10.3 %all-gather.2 = bf16[4,2,2048]{2,1,0:T(2,128)(2,1)S(1)} all-gather(bf16[1,2,2048]{2,1,0:T(2,128)(2,1)S(1)} %reshape.350), channel_id=1, replica_groups=mesh['section'=4,'row'=2,'col'=4] {'col'}, dimensions={0}, use_global_device_ids=true | all-gather | bytes 40960 | tf_op jit(solution)/shard_map/while/body/eval_jaxpr/all_gather | solution.py:89
  60.5 2.8 fusion.77
  63.3 6.3 %psum.16 = f32[8,1024]{1,0:T(8,128)S(1)} all-reduce(f32[8,1024]{1,0:T(8,128)S(1)} %fusion.77), channel_id=1, replica_groups=mesh['section'=4,'row'=2,'col'=4] {'row'}, use_global_device_ids=true, to_apply=%region_6.6 | all-reduce | flops 8192 | bytes 65536 | tf_op jit(solution)/shard_map/while/body/eval_jaxpr/psum | solution.py:93
  69.6 10.6 %collective-permute-start = (bf16[8,1024]{1,0:T(8,128)(2,1)S(1)}, bf16[8,1024]{1,0:T(8,128)(2,1)S(1)}, u32[]{:S(2)}, u32[]{:S(2)}) collective-permute-start(bf16[8,1024]{1,0:T(8,128)(2,1)S(1)} %get-tuple-element.491), channel_id=1, source_target_pairs={{0,8},{8,16},{16,24},{1,9},{9,17},{17,25},{2,10},{10,18},{18,26},{... | collective-permute-start | bytes 49160 | tf_op jit(solution)/shard_map/while/body/eval_jaxpr/ppermute | solution.py:14
  82.0 4.3 fusion.65
  86.7 8.6 %all-reduce.5 = f32[8]{0:T(128)S(1)} all-reduce(f32[8]{0:T(128)S(1)} %get-tuple-element.477), channel_id=3, replica_groups=mesh['section'=4,'row'=2,'col'=4] {'col'}, use_global_device_ids=true, to_apply=%region_3.3.clone | all-reduce | flops 8 | bytes 64 | tf_op jit(solution)/shard_map/while
  96.4 1.2 constant_dynamic-slice_fusion.7
  97.7 20.6 %all-reduce.8.cloned.1.call-done = f32[8,3072]{1,0:T(8,128)} async-done(((f32[8,3072]{1,0:T(8,128)}), f32[8,3072]{1,0:T(8,128)}) %all-reduce.8.cloned.1.call-update) | async-done | bytes 98320 | tf_op jit(solution)/shard_map/while
  118.3 1.0 dynamic-slice_multiply_fusion.3
  120.5 10.3 %all-gather.2 = bf16[4,2,2048]{2,1,0:T(2,128)(2,1)S(1)} all-gather(bf16[1,2,2048]{2,1,0:T(2,128)(2,1)S(1)} %reshape.350), channel_id=1, replica_groups=mesh['section'=4,'row'=2,'col'=4] {'col'}, dimensions={0}, use_global_device_ids=true | all-gather | bytes 40960 | tf_op jit(solution)/shard_map/while/body/eval_jaxpr/all_gather | solution.py:89
  130.8 2.8 fusion.77
  133.6 6.3 %psum.16 = f32[8,1024]{1,0:T(8,128)S(1)} all-reduce(f32[8,1024]{1,0:T(8,128)S(1)} %fusion.77), channel_id=1, replica_groups=mesh['section'=4,'row'=2,'col'=4] {'row'}, use_global_device_ids=true, to_apply=%region_6.6 | all-reduce | flops 8192 | bytes 65536 | tf_op jit(solution)/shard_map/while/body/eval_jaxpr/psum | solution.py:93
  140.0 10.6 %collective-permute-start = (bf16[8,1024]{1,0:T(8,128)(2,1)S(1)}, bf16[8,1024]{1,0:T(8,128)(2,1)S(1)}, u32[]{:S(2)}, u32[]{:S(2)}) collective-permute-start(bf16[8,1024]{1,0:T(8,128)(2,1)S(1)} %get-tuple-element.491), channel_id=1, source_target_pairs={{0,8},{8,16},{16,24},{1,9},{9,17},{17,25},{2,10},{10,18},{18,26},{... | collective-permute-start | bytes 49160 | tf_op jit(solution)/shard_map/while/body/eval_jaxpr/ppermute | solution.py:14
  152.3 4.3 fusion.65
  157.0 8.6 %all-reduce.5 = f32[8]{0:T(128)S(1)} all-reduce(f32[8]{0:T(128)S(1)} %get-tuple-element.477), channel_id=3, replica_groups=mesh['section'=4,'row'=2,'col'=4] {'col'}, use_global_device_ids=true, to_apply=%region_3.3.clone | all-reduce | flops 8 | bytes 64 | tf_op jit(solution)/shard_map/while
  166.7 1.2 constant_dynamic-slice_fusion.7
  168.0 20.5 %all-reduce.8.cloned.1.call-done = f32[8,3072]{1,0:T(8,128)} async-done(((f32[8,3072]{1,0:T(8,128)}), f32[8,3072]{1,0:T(8,128)}) %all-reduce.8.cloned.1.call-update) | async-done | bytes 98320 | tf_op jit(solution)/shard_map/while
  188.6 1.0 dynamic-slice_multiply_fusion.3
  190.8 10.3 %all-gather.2 = bf16[4,2,2048]{2,1,0:T(2,128)(2,1)S(1)} all-gather(bf16[1,2,2048]{2,1,0:T(2,128)(2,1)S(1)} %reshape.350), channel_id=1, replica_groups=mesh['section'=4,'row'=2,'col'=4] {'col'}, dimensions={0}, use_global_device_ids=true | all-gather | bytes 40960 | tf_op jit(solution)/shard_map/while/body/eval_jaxpr/all_gather | solution.py:89
  201.1 2.8 fusion.77
  204.0 6.3 %psum.16 = f32[8,1024]{1,0:T(8,128)S(1)} all-reduce(f32[8,1024]{1,0:T(8,128)S(1)} %fusion.77), channel_id=1, replica_groups=mesh['section'=4,'row'=2,'col'=4] {'row'}, use_global_device_ids=true, to_apply=%region_6.6 | all-reduce | flops 8192 | bytes 65536 | tf_op jit(solution)/shard_map/while/body/eval_jaxpr/psum | solution.py:93
  210.3 10.6 %collective-permute-start = (bf16[8,1024]{1,0:T(8,128)(2,1)S(1)}, bf16[8,1024]{1,0:T(8,128)(2,1)S(1)}, u32[]{:S(2)}, u32[]{:S(2)}) collective-permute-start(bf16[8,1024]{1,0:T(8,128)(2,1)S(1)} %get-tuple-element.491), channel_id=1, source_target_pairs={{0,8},{8,16},{16,24},{1,9},{9,17},{17,25},{2,10},{10,18},{18,26},{... | collective-permute-start | bytes 49160 | tf_op jit(solution)/shard_map/while/body/eval_jaxpr/ppermute | solution.py:14
  222.6 4.3 fusion.65
  227.3 8.6 %all-reduce.5 = f32[8]{0:T(128)S(1)} all-reduce(f32[8]{0:T(128)S(1)} %get-tuple-element.477), channel_id=3, replica_groups=mesh['section'=4,'row'=2,'col'=4] {'col'}, use_global_device_ids=true, to_apply=%region_3.3.clone | all-reduce | flops 8 | bytes 64 | tf_op jit(solution)/shard_map/while
  237.0 1.2 constant_dynamic-slice_fusion.7
  238.3 20.5 %all-reduce.8.cloned.1.call-done = f32[8,3072]{1,0:T(8,128)} async-done(((f32[8,3072]{1,0:T(8,128)}), f32[8,3072]{1,0:T(8,128)}) %all-reduce.8.cloned.1.call-update) | async-done | bytes 98320 | tf_op jit(solution)/shard_map/while
  258.9 1.0 dynamic-slice_multiply_fusion.3
  261.2 10.3 %all-gather.2 = bf16[4,2,2048]{2,1,0:T(2,128)(2,1)S(1)} all-gather(bf16[1,2,2048]{2,1,0:T(2,128)(2,1)S(1)} %reshape.350), channel_id=1, replica_groups=mesh['section'=4,'row'=2,'col'=4] {'col'}, dimensions={0}, use_global_device_ids=true | all-gather | bytes 40960 | tf_op jit(solution)/shard_map/while/body/eval_jaxpr/all_gather | solution.py:89
  271.4 2.8 fusion.77
  274.3 6.3 %psum.16 = f32[8,1024]{1,0:T(8,128)S(1)} all-reduce(f32[8,1024]{1,0:T(8,128)S(1)} %fusion.77), channel_id=1, replica_groups=mesh['section'=4,'row'=2,'col'=4] {'row'}, use_global_device_ids=true, to_apply=%region_6.6 | all-reduce | flops 8192 | bytes 65536 | tf_op jit(solution)/shard_map/while/body/eval_jaxpr/psum | solution.py:93
  280.6 10.6 %collective-permute-start = (bf16[8,1024]{1,0:T(8,128)(2,1)S(1)}, bf16[8,1024]{1,0:T(8,128)(2,1)S(1)}, u32[]{:S(2)}, u32[]{:S(2)}) collective-permute-start(bf16[8,1024]{1,0:T(8,128)(2,1)S(1)} %get-tuple-element.491), channel_id=1, source_target_pairs={{0,8},{8,16},{16,24},{1,9},{9,17},{17,25},{2,10},{10,18},{18,26},{... | collective-permute-start | bytes 49160 | tf_op jit(solution)/shard_map/while/body/eval_jaxpr/ppermute | solution.py:14
  292.9 4.3 fusion.65
  297.6 8.6 %all-reduce.5 = f32[8]{0:T(128)S(1)} all-reduce(f32[8]{0:T(128)S(1)} %get-tuple-element.477), channel_id=3, replica_groups=mesh['section'=4,'row'=2,'col'=4] {'col'}, use_global_device_ids=true, to_apply=%region_3.3.clone | all-reduce | flops 8 | bytes 64 | tf_op jit(solution)/shard_map/while
  307.4 1.2 constant_dynamic-slice_fusion.7
  308.7 20.5 %all-reduce.8.cloned.1.call-done = f32[8,3072]{1,0:T(8,128)} async-done(((f32[8,3072]{1,0:T(8,128)}), f32[8,3072]{1,0:T(8,128)}) %all-reduce.8.cloned.1.call-update) | async-done | bytes 98320 | tf_op jit(solution)/shard_map/while
  329.2 1.0 dynamic-slice_multiply_fusion.3
  331.5 10.3 %all-gather.2 = bf16[4,2,2048]{2,1,0:T(2,128)(2,1)S(1)} all-gather(bf16[1,2,2048]{2,1,0:T(2,128)(2,1)S(1)} %reshape.350), channel_id=1, replica_groups=mesh['section'=4,'row'=2,'col'=4] {'col'}, dimensions={0}, use_global_device_ids=true | all-gather | bytes 40960 | tf_op jit(solution)/shard_map/while/body/eval_jaxpr/all_gather | solution.py:89
  341.8 2.8 fusion.77
  344.6 6.3 %psum.16 = f32[8,1024]{1,0:T(8,128)S(1)} all-reduce(f32[8,1024]{1,0:T(8,128)S(1)} %fusion.77), channel_id=1, replica_groups=mesh['section'=4,'row'=2,'col'=4] {'row'}, use_global_device_ids=true, to_apply=%region_6.6 | all-reduce | flops 8192 | bytes 65536 | tf_op jit(solution)/shard_map/while/body/eval_jaxpr/psum | solution.py:93
  350.9 10.6 %collective-permute-start = (bf16[8,1024]{1,0:T(8,128)(2,1)S(1)}, bf16[8,1024]{1,0:T(8,128)(2,1)S(1)}, u32[]{:S(2)}, u32[]{:S(2)}) collective-permute-start(bf16[8,1024]{1,0:T(8,128)(2,1)S(1)} %get-tuple-element.491), channel_id=1, source_target_pairs={{0,8},{8,16},{16,24},{1,9},{9,17},{17,25},{2,10},{10,18},{18,26},{... | collective-permute-start | bytes 49160 | tf_op jit(solution)/shard_map/while/body/eval_jaxpr/ppermute | solution.py:14
  363.3 4.3 fusion.65
  368.0 8.6 %all-reduce.5 = f32[8]{0:T(128)S(1)} all-reduce(f32[8]{0:T(128)S(1)} %get-tuple-element.477), channel_id=3, replica_groups=mesh['section'=4,'row'=2,'col'=4] {'col'}, use_global_device_ids=true, to_apply=%region_3.3.clone | all-reduce | flops 8 | bytes 64 | tf_op jit(solution)/shard_map/while
  377.7 1.2 constant_dynamic-slice_fusion.7
  379.0 20.5 %all-reduce.8.cloned.1.call-done = f32[8,3072]{1,0:T(8,128)} async-done(((f32[8,3072]{1,0:T(8,128)}), f32[8,3072]{1,0:T(8,128)}) %all-reduce.8.cloned.1.call-update) | async-done | bytes 98320 | tf_op jit(solution)/shard_map/while
  399.5 1.0 dynamic-slice_multiply_fusion.3
  401.8 10.3 %all-gather.2 = bf16[4,2,2048]{2,1,0:T(2,128)(2,1)S(1)} all-gather(bf16[1,2,2048]{2,1,0:T(2,128)(2,1)S(1)} %reshape.350), channel_id=1, replica_groups=mesh['section'=4,'row'=2,'col'=4] {'col'}, dimensions={0}, use_global_device_ids=true | all-gather | bytes 40960 | tf_op jit(solution)/shard_map/while/body/eval_jaxpr/all_gather | solution.py:89
  412.1 2.8 fusion.77
  414.9 6.3 %psum.16 = f32[8,1024]{1,0:T(8,128)S(1)} all-reduce(f32[8,1024]{1,0:T(8,128)S(1)} %fusion.77), channel_id=1, replica_groups=mesh['section'=4,'row'=2,'col'=4] {'row'}, use_global_device_ids=true, to_apply=%region_6.6 | all-reduce | flops 8192 | bytes 65536 | tf_op jit(solution)/shard_map/while/body/eval_jaxpr/psum | solution.py:93
  421.2 10.6 %collective-permute-start = (bf16[8,1024]{1,0:T(8,128)(2,1)S(1)}, bf16[8,1024]{1,0:T(8,128)(2,1)S(1)}, u32[]{:S(2)}, u32[]{:S(2)}) collective-permute-start(bf16[8,1024]{1,0:T(8,128)(2,1)S(1)} %get-tuple-element.491), channel_id=1, source_target_pairs={{0,8},{8,16},{16,24},{1,9},{9,17},{17,25},{2,10},{10,18},{18,26},{... | collective-permute-start | bytes 49160 | tf_op jit(solution)/shard_map/while/body/eval_jaxpr/ppermute | solution.py:14
  433.6 4.3 fusion.65
  438.3 8.6 %all-reduce.5 = f32[8]{0:T(128)S(1)} all-reduce(f32[8]{0:T(128)S(1)} %get-tuple-element.477), channel_id=3, replica_groups=mesh['section'=4,'row'=2,'col'=4] {'col'}, use_global_device_ids=true, to_apply=%region_3.3.clone | all-reduce | flops 8 | bytes 64 | tf_op jit(solution)/shard_map/while
  448.0 1.2 constant_dynamic-slice_fusion.7
  449.3 20.5 %all-reduce.8.cloned.1.call-done = f32[8,3072]{1,0:T(8,128)} async-done(((f32[8,3072]{1,0:T(8,128)}), f32[8,3072]{1,0:T(8,128)}) %all-reduce.8.cloned.1.call-update) | async-done | bytes 98320 | tf_op jit(solution)/shard_map/while
  469.9 1.0 dynamic-slice_multiply_fusion.3
  472.1 10.3 %all-gather.2 = bf16[4,2,2048]{2,1,0:T(2,128)(2,1)S(1)} all-gather(bf16[1,2,2048]{2,1,0:T(2,128)(2,1)S(1)} %reshape.350), channel_id=1, replica_groups=mesh['section'=4,'row'=2,'col'=4] {'col'}, dimensions={0}, use_global_device_ids=true | all-gather | bytes 40960 | tf_op jit(solution)/shard_map/while/body/eval_jaxpr/all_gather | solution.py:89
  482.4 2.8 fusion.77
  485.2 6.3 %psum.16 = f32[8,1024]{1,0:T(8,128)S(1)} all-reduce(f32[8,1024]{1,0:T(8,128)S(1)} %fusion.77), channel_id=1, replica_groups=mesh['section'=4,'row'=2,'col'=4] {'row'}, use_global_device_ids=true, to_apply=%region_6.6 | all-reduce | flops 8192 | bytes 65536 | tf_op jit(solution)/shard_map/while/body/eval_jaxpr/psum | solution.py:93
  491.6 10.6 %collective-permute-start = (bf16[8,1024]{1,0:T(8,128)(2,1)S(1)}, bf16[8,1024]{1,0:T(8,128)(2,1)S(1)}, u32[]{:S(2)}, u32[]{:S(2)}) collective-permute-start(bf16[8,1024]{1,0:T(8,128)(2,1)S(1)} %get-tuple-element.491), channel_id=1, source_target_pairs={{0,8},{8,16},{16,24},{1,9},{9,17},{17,25},{2,10},{10,18},{18,26},{... | collective-permute-start | bytes 49160 | tf_op jit(solution)/shard_map/while/body/eval_jaxpr/ppermute | solution.py:14
  (223 shorter events, 29.9 us)
Async XLA Ops:
  8.0 16.4 %copy-start.1 = (u32[32]{0:T(128)S(1)}, u32[32]{0:T(128)}, u32[]{:S(2)}) copy-start(u32[32]{0:T(128)} %get-tuple-element.547) | copy-start | bytes 388 | tf_op jit(solution)/shard_map/while
  8.0 39.9 %all-reduce.8.cloned.1.call-start = ((), (), s32[]{:S(2)}) async-start(), calls=%async_computation | async-start | bytes 196608 | tf_op jit(solution)/shard_map/while
  69.6 11.5 %collective-permute-start = (bf16[8,1024]{1,0:T(8,128)(2,1)S(1)}, bf16[8,1024]{1,0:T(8,128)(2,1)S(1)}, u32[]{:S(2)}, u32[]{:S(2)}) collective-permute-start(bf16[8,1024]{1,0:T(8,128)(2,1)S(1)} %get-tuple-element.491), channel_id=1, source_target_pairs={{0,8},{8,16},{16,24},{1,9},{9,17},{17,25},{2,10},{10,18},{18,26},{... | collective-permute-start | bytes 49160 | tf_op jit(solution)/shard_map/while/body/eval_jaxpr/ppermute | solution.py:14
  81.1 14.1 %copy-start.1 = (u32[32]{0:T(128)S(1)}, u32[32]{0:T(128)}, u32[]{:S(2)}) copy-start(u32[32]{0:T(128)} %get-tuple-element.547) | copy-start | bytes 388 | tf_op jit(solution)/shard_map/while
  81.1 37.1 %all-reduce.8.cloned.1.call-start = ((), (), s32[]{:S(2)}) async-start(), calls=%async_computation | async-start | bytes 196608 | tf_op jit(solution)/shard_map/while
  140.0 11.5 %collective-permute-start = (bf16[8,1024]{1,0:T(8,128)(2,1)S(1)}, bf16[8,1024]{1,0:T(8,128)(2,1)S(1)}, u32[]{:S(2)}, u32[]{:S(2)}) collective-permute-start(bf16[8,1024]{1,0:T(8,128)(2,1)S(1)} %get-tuple-element.491), channel_id=1, source_target_pairs={{0,8},{8,16},{16,24},{1,9},{9,17},{17,25},{2,10},{10,18},{18,26},{... | collective-permute-start | bytes 49160 | tf_op jit(solution)/shard_map/while/body/eval_jaxpr/ppermute | solution.py:14
  151.4 14.1 %copy-start.1 = (u32[32]{0:T(128)S(1)}, u32[32]{0:T(128)}, u32[]{:S(2)}) copy-start(u32[32]{0:T(128)} %get-tuple-element.547) | copy-start | bytes 388 | tf_op jit(solution)/shard_map/while
  151.4 37.1 %all-reduce.8.cloned.1.call-start = ((), (), s32[]{:S(2)}) async-start(), calls=%async_computation | async-start | bytes 196608 | tf_op jit(solution)/shard_map/while
  210.3 11.5 %collective-permute-start = (bf16[8,1024]{1,0:T(8,128)(2,1)S(1)}, bf16[8,1024]{1,0:T(8,128)(2,1)S(1)}, u32[]{:S(2)}, u32[]{:S(2)}) collective-permute-start(bf16[8,1024]{1,0:T(8,128)(2,1)S(1)} %get-tuple-element.491), channel_id=1, source_target_pairs={{0,8},{8,16},{16,24},{1,9},{9,17},{17,25},{2,10},{10,18},{18,26},{... | collective-permute-start | bytes 49160 | tf_op jit(solution)/shard_map/while/body/eval_jaxpr/ppermute | solution.py:14
  221.8 14.1 %copy-start.1 = (u32[32]{0:T(128)S(1)}, u32[32]{0:T(128)}, u32[]{:S(2)}) copy-start(u32[32]{0:T(128)} %get-tuple-element.547) | copy-start | bytes 388 | tf_op jit(solution)/shard_map/while
  221.8 37.1 %all-reduce.8.cloned.1.call-start = ((), (), s32[]{:S(2)}) async-start(), calls=%async_computation | async-start | bytes 196608 | tf_op jit(solution)/shard_map/while
  280.6 11.5 %collective-permute-start = (bf16[8,1024]{1,0:T(8,128)(2,1)S(1)}, bf16[8,1024]{1,0:T(8,128)(2,1)S(1)}, u32[]{:S(2)}, u32[]{:S(2)}) collective-permute-start(bf16[8,1024]{1,0:T(8,128)(2,1)S(1)} %get-tuple-element.491), channel_id=1, source_target_pairs={{0,8},{8,16},{16,24},{1,9},{9,17},{17,25},{2,10},{10,18},{18,26},{... | collective-permute-start | bytes 49160 | tf_op jit(solution)/shard_map/while/body/eval_jaxpr/ppermute | solution.py:14
  292.1 14.1 %copy-start.1 = (u32[32]{0:T(128)S(1)}, u32[32]{0:T(128)}, u32[]{:S(2)}) copy-start(u32[32]{0:T(128)} %get-tuple-element.547) | copy-start | bytes 388 | tf_op jit(solution)/shard_map/while
  292.1 37.1 %all-reduce.8.cloned.1.call-start = ((), (), s32[]{:S(2)}) async-start(), calls=%async_computation | async-start | bytes 196608 | tf_op jit(solution)/shard_map/while
  350.9 11.5 %collective-permute-start = (bf16[8,1024]{1,0:T(8,128)(2,1)S(1)}, bf16[8,1024]{1,0:T(8,128)(2,1)S(1)}, u32[]{:S(2)}, u32[]{:S(2)}) collective-permute-start(bf16[8,1024]{1,0:T(8,128)(2,1)S(1)} %get-tuple-element.491), channel_id=1, source_target_pairs={{0,8},{8,16},{16,24},{1,9},{9,17},{17,25},{2,10},{10,18},{18,26},{... | collective-permute-start | bytes 49160 | tf_op jit(solution)/shard_map/while/body/eval_jaxpr/ppermute | solution.py:14
  362.4 14.1 %copy-start.1 = (u32[32]{0:T(128)S(1)}, u32[32]{0:T(128)}, u32[]{:S(2)}) copy-start(u32[32]{0:T(128)} %get-tuple-element.547) | copy-start | bytes 388 | tf_op jit(solution)/shard_map/while
  362.4 37.1 %all-reduce.8.cloned.1.call-start = ((), (), s32[]{:S(2)}) async-start(), calls=%async_computation | async-start | bytes 196608 | tf_op jit(solution)/shard_map/while
  421.2 11.5 %collective-permute-start = (bf16[8,1024]{1,0:T(8,128)(2,1)S(1)}, bf16[8,1024]{1,0:T(8,128)(2,1)S(1)}, u32[]{:S(2)}, u32[]{:S(2)}) collective-permute-start(bf16[8,1024]{1,0:T(8,128)(2,1)S(1)} %get-tuple-element.491), channel_id=1, source_target_pairs={{0,8},{8,16},{16,24},{1,9},{9,17},{17,25},{2,10},{10,18},{18,26},{... | collective-permute-start | bytes 49160 | tf_op jit(solution)/shard_map/while/body/eval_jaxpr/ppermute | solution.py:14
  432.7 14.1 %copy-start.1 = (u32[32]{0:T(128)S(1)}, u32[32]{0:T(128)}, u32[]{:S(2)}) copy-start(u32[32]{0:T(128)} %get-tuple-element.547) | copy-start | bytes 388 | tf_op jit(solution)/shard_map/while
  432.7 37.1 %all-reduce.8.cloned.1.call-start = ((), (), s32[]{:S(2)}) async-start(), calls=%async_computation | async-start | bytes 196608 | tf_op jit(solution)/shard_map/while
  491.6 11.5 %collective-permute-start = (bf16[8,1024]{1,0:T(8,128)(2,1)S(1)}, bf16[8,1024]{1,0:T(8,128)(2,1)S(1)}, u32[]{:S(2)}, u32[]{:S(2)}) collective-permute-start(bf16[8,1024]{1,0:T(8,128)(2,1)S(1)} %get-tuple-element.491), channel_id=1, source_target_pairs={{0,8},{8,16},{16,24},{1,9},{9,17},{17,25},{2,10},{10,18},{18,26},{... | collective-permute-start | bytes 49160 | tf_op jit(solution)/shard_map/while/body/eval_jaxpr/ppermute | solution.py:14
  503.0 0.6 copy-start
Sparse Core Ops, SparseCore 0:
  13.5 34.4 all-reduce.7
  86.5 31.7 all-reduce.7
  156.8 31.7 all-reduce.7
  227.1 31.7 all-reduce.7
  297.4 31.7 all-reduce.7
  367.7 31.7 all-reduce.7
  438.1 31.7 all-reduce.7
where the time goes:
time: 512 us; the launch traced here: 511 us
  blocking collectives  178 us (35%)
  waiting for transfers between devices  150 us (29%)
  starting transfers between devices  74.5 us (15%)
  matrix products  55 us (11%)
  other arithmetic  19.8 us (4%)
  local copies, waits for them, and re-layouts  14.6 us (3%)
  between operations  13.4 us (3%)
    while x14, waiting for transfers between devices  144 us
    ppermute x7, starting transfers between devices, from_behind(): return lax.ppermute(x, axis, pairs)  74.4 us
    all_gather x7, blocking collectives, layer_part(): lax.all_gather(attended, 'col', axis=0, tiled=True)  71.8 us
    while x7, blocking collectives  62.2 us
    psum x7, blocking collectives, layer_part(): summed = lax.psum(mixed_rows, 'row')  44 us
    dot_general x7, matrix products, layer_part(): jnp.dot(scaled, proj_weight, preferred_element_type=jnp.float32)  30.4 us
    dot_general x7, matrix products, layer_part(): jnp.dot(lax.all_gather(attended, 'col', axis=0, tiled=True), out_weight,...  19.9 us
  transfers between devices with their start and end apart: 14, of which 14 were waited for; matrix products, arithmetic and copies ran while one was open for 3% of the time, Pallas kernels for 0%

commit v1 on v0

--- a/solution.py
+++ b/solution.py
@@ -90,7 +90,7 @@
             out_weight,
             preferred_element_type=jnp.float32,
         )
-        summed = lax.psum(mixed_rows, "row")
+        summed = jnp.sum(lax.all_gather(mixed_rows, "row"), axis=0)
         return (h_float + summed).astype(jnp.bfloat16)
 
     def advance(tick_at, loop_state):

time: 512 us -> 492 us (0.961)
  blocking collectives: 178 us -> 158 us
  starting transfers between devices: 74.5 us -> 68.4 us
  waiting for transfers between devices: 150 us -> 156 us
    psum x7 -> x0, blocking collectives: 44 us -> none  [layer_part(): summed = lax.psum(mixed_rows, 'row')]
    all_gather x0 -> x7, blocking collectives: none -> 24 us  [layer_part(): summed = jnp.sum(lax.all_gather(mixed_rows, 'row'), axis=0)]
    ppermute x7, starting transfers between devices: 74.4 us -> 68.3 us  [from_behind(): return lax.ppermute(x, axis, pairs)]
    while x14, waiting for transfers between devices: 144 us -> 150 us
where the time goes in v1:
time: 492 us; the launch traced here: 490 us
  blocking collectives  158 us (32%)
  waiting for transfers between devices  156 us (32%)
  starting transfers between devices  68.4 us (14%)
  matrix products  55 us (11%)
  other arithmetic  19.8 us (4%)
  local copies, waits for them, and re-layouts  14.6 us (3%)
  between operations  13.4 us (3%)
    while x14, waiting for transfers between devices  150 us
    all_gather x7, blocking collectives, layer_part(): lax.all_gather(attended, 'col', axis=0, tiled=True)  71.8 us
    ppermute x7, starting transfers between devices, from_behind(): return lax.ppermute(x, axis, pairs)  68.3 us
    while x7, blocking collectives  62.3 us
    dot_general x7, matrix products, layer_part(): jnp.dot(scaled, proj_weight, preferred_element_type=jnp.float32)  30.4 us
    all_gather x7, blocking collectives, layer_part(): summed = jnp.sum(lax.all_gather(mixed_rows, 'row'), axis=0)  24 us
    dot_general x7, matrix products, layer_part(): jnp.dot(lax.all_gather(attended, 'col', axis=0, tiled=True), out_weight,...  19.9 us
  transfers between devices with their start and end apart: 14, of which 14 were waited for; matrix products, arithmetic and copies ran while one was open for 3% of the time, Pallas kernels for 0%

profile of v1, /device:TPU:1, one launch (start us, length us, event | category | flops | bytes accessed | tf_op | source)
XLA Modules:
  0.0 490.0 jit_solution(1584635352629555875)
XLA Ops:
  8.0 474.5 %while.18 = (s32[]{:T(128)}, bf16[8,1024]{1,0:T(8,128)(2,1)S(1)}, bf16[4,8,1024]{2,1,0:T(8,128)(2,1)S(1)}, pred[]{:T(512)}, bf16[4,8,1024]{2,1,0:T(8,128)(2,1)},...) while((s32[]{:T(128)}, bf16[8,1024]{1,0:T(8,128)(2,1)S(1)}, ...), condition=%wide.region_7.8_spmd, body=%wide.region_0.7_spmd.sunk | while | flops 86196720 | bytes 13700056 | solution.py:117
  9.0 4.3 fusion.65
  13.7 10.8 %all-reduce.5 = f32[8]{0:T(128)S(1)} all-reduce(f32[8]{0:T(128)S(1)} %get-tuple-element.477), channel_id=4, replica_groups=mesh['section'=4,'row'=2,'col'=4] {'col'}, use_global_device_ids=true, to_apply=%region_3.3.clone | all-reduce | flops 8 | bytes 64 | tf_op jit(solution)/shard_map/while
  25.6 1.2 constant_dynamic-slice_fusion.7
  26.9 21.0 %all-reduce.8.cloned.1.call-done = f32[8,3072]{1,0:T(8,128)} async-done(((f32[8,3072]{1,0:T(8,128)}), f32[8,3072]{1,0:T(8,128)}) %all-reduce.8.cloned.1.call-update) | async-done | bytes 98320 | tf_op jit(solution)/shard_map/while
  47.9 1.0 dynamic-slice_multiply_fusion.3
  50.2 10.3 %all-gather.4 = bf16[4,2,2048]{2,1,0:T(2,128)(2,1)S(1)} all-gather(bf16[1,2,2048]{2,1,0:T(2,128)(2,1)S(1)} %reshape.351), channel_id=1, replica_groups=mesh['section'=4,'row'=2,'col'=4] {'col'}, dimensions={0}, use_global_device_ids=true | all-gather | bytes 40960 | tf_op jit(solution)/shard_map/while/body/eval_jaxpr/all_gather | solution.py:89
  60.5 2.8 fusion.77
  63.3 3.4 all-gather.5
  66.8 9.8 %collective-permute-start = (bf16[8,1024]{1,0:T(8,128)(2,1)S(1)}, bf16[8,1024]{1,0:T(8,128)(2,1)S(1)}, u32[]{:S(2)}, u32[]{:S(2)}) collective-permute-start(bf16[8,1024]{1,0:T(8,128)(2,1)S(1)} %get-tuple-element.491), channel_id=1, source_target_pairs={{0,8},{8,16},{16,24},{1,9},{9,17},{17,25},{2,10},{10,18},{18,26},{... | collective-permute-start | bytes 49160 | tf_op jit(solution)/shard_map/while/body/eval_jaxpr/ppermute | solution.py:14
  78.2 4.3 fusion.65
  82.9 8.6 %all-reduce.5 = f32[8]{0:T(128)S(1)} all-reduce(f32[8]{0:T(128)S(1)} %get-tuple-element.477), channel_id=4, replica_groups=mesh['section'=4,'row'=2,'col'=4] {'col'}, use_global_device_ids=true, to_apply=%region_3.3.clone | all-reduce | flops 8 | bytes 64 | tf_op jit(solution)/shard_map/while
  92.7 1.2 constant_dynamic-slice_fusion.7
  94.0 21.5 %all-reduce.8.cloned.1.call-done = f32[8,3072]{1,0:T(8,128)} async-done(((f32[8,3072]{1,0:T(8,128)}), f32[8,3072]{1,0:T(8,128)}) %all-reduce.8.cloned.1.call-update) | async-done | bytes 98320 | tf_op jit(solution)/shard_map/while
  115.5 1.0 dynamic-slice_multiply_fusion.3
  117.7 10.3 %all-gather.4 = bf16[4,2,2048]{2,1,0:T(2,128)(2,1)S(1)} all-gather(bf16[1,2,2048]{2,1,0:T(2,128)(2,1)S(1)} %reshape.351), channel_id=1, replica_groups=mesh['section'=4,'row'=2,'col'=4] {'col'}, dimensions={0}, use_global_device_ids=true | all-gather | bytes 40960 | tf_op jit(solution)/shard_map/while/body/eval_jaxpr/all_gather | solution.py:89
  128.0 2.8 fusion.77
  130.8 3.4 all-gather.5
  134.3 9.8 %collective-permute-start = (bf16[8,1024]{1,0:T(8,128)(2,1)S(1)}, bf16[8,1024]{1,0:T(8,128)(2,1)S(1)}, u32[]{:S(2)}, u32[]{:S(2)}) collective-permute-start(bf16[8,1024]{1,0:T(8,128)(2,1)S(1)} %get-tuple-element.491), channel_id=1, source_target_pairs={{0,8},{8,16},{16,24},{1,9},{9,17},{17,25},{2,10},{10,18},{18,26},{... | collective-permute-start | bytes 49160 | tf_op jit(solution)/shard_map/while/body/eval_jaxpr/ppermute | solution.py:14
  145.7 4.3 fusion.65
  150.4 8.6 %all-reduce.5 = f32[8]{0:T(128)S(1)} all-reduce(f32[8]{0:T(128)S(1)} %get-tuple-element.477), channel_id=4, replica_groups=mesh['section'=4,'row'=2,'col'=4] {'col'}, use_global_device_ids=true, to_apply=%region_3.3.clone | all-reduce | flops 8 | bytes 64 | tf_op jit(solution)/shard_map/while
  160.2 1.2 constant_dynamic-slice_fusion.7
  161.5 21.5 %all-reduce.8.cloned.1.call-done = f32[8,3072]{1,0:T(8,128)} async-done(((f32[8,3072]{1,0:T(8,128)}), f32[8,3072]{1,0:T(8,128)}) %all-reduce.8.cloned.1.call-update) | async-done | bytes 98320 | tf_op jit(solution)/shard_map/while
  183.0 1.0 dynamic-slice_multiply_fusion.3
  185.2 10.3 %all-gather.4 = bf16[4,2,2048]{2,1,0:T(2,128)(2,1)S(1)} all-gather(bf16[1,2,2048]{2,1,0:T(2,128)(2,1)S(1)} %reshape.351), channel_id=1, replica_groups=mesh['section'=4,'row'=2,'col'=4] {'col'}, dimensions={0}, use_global_device_ids=true | all-gather | bytes 40960 | tf_op jit(solution)/shard_map/while/body/eval_jaxpr/all_gather | solution.py:89
  195.5 2.8 fusion.77
  198.4 3.4 all-gather.5
  201.8 9.8 %collective-permute-start = (bf16[8,1024]{1,0:T(8,128)(2,1)S(1)}, bf16[8,1024]{1,0:T(8,128)(2,1)S(1)}, u32[]{:S(2)}, u32[]{:S(2)}) collective-permute-start(bf16[8,1024]{1,0:T(8,128)(2,1)S(1)} %get-tuple-element.491), channel_id=1, source_target_pairs={{0,8},{8,16},{16,24},{1,9},{9,17},{17,25},{2,10},{10,18},{18,26},{... | collective-permute-start | bytes 49160 | tf_op jit(solution)/shard_map/while/body/eval_jaxpr/ppermute | solution.py:14
  213.3 4.3 fusion.65
  218.0 8.6 %all-reduce.5 = f32[8]{0:T(128)S(1)} all-reduce(f32[8]{0:T(128)S(1)} %get-tuple-element.477), channel_id=4, replica_groups=mesh['section'=4,'row'=2,'col'=4] {'col'}, use_global_device_ids=true, to_apply=%region_3.3.clone | all-reduce | flops 8 | bytes 64 | tf_op jit(solution)/shard_map/while
  227.7 1.2 constant_dynamic-slice_fusion.7
  229.0 21.5 %all-reduce.8.cloned.1.call-done = f32[8,3072]{1,0:T(8,128)} async-done(((f32[8,3072]{1,0:T(8,128)}), f32[8,3072]{1,0:T(8,128)}) %all-reduce.8.cloned.1.call-update) | async-done | bytes 98320 | tf_op jit(solution)/shard_map/while
  250.5 1.0 dynamic-slice_multiply_fusion.3
  252.8 10.3 %all-gather.4 = bf16[4,2,2048]{2,1,0:T(2,128)(2,1)S(1)} all-gather(bf16[1,2,2048]{2,1,0:T(2,128)(2,1)S(1)} %reshape.351), channel_id=1, replica_groups=mesh['section'=4,'row'=2,'col'=4] {'col'}, dimensions={0}, use_global_device_ids=true | all-gather | bytes 40960 | tf_op jit(solution)/shard_map/while/body/eval_jaxpr/all_gather | solution.py:89
  263.0 2.8 fusion.77
  265.9 3.4 all-gather.5
  269.3 9.8 %collective-permute-start = (bf16[8,1024]{1,0:T(8,128)(2,1)S(1)}, bf16[8,1024]{1,0:T(8,128)(2,1)S(1)}, u32[]{:S(2)}, u32[]{:S(2)}) collective-permute-start(bf16[8,1024]{1,0:T(8,128)(2,1)S(1)} %get-tuple-element.491), channel_id=1, source_target_pairs={{0,8},{8,16},{16,24},{1,9},{9,17},{17,25},{2,10},{10,18},{18,26},{... | collective-permute-start | bytes 49160 | tf_op jit(solution)/shard_map/while/body/eval_jaxpr/ppermute | solution.py:14
  280.8 4.3 fusion.65
  285.5 8.6 %all-reduce.5 = f32[8]{0:T(128)S(1)} all-reduce(f32[8]{0:T(128)S(1)} %get-tuple-element.477), channel_id=4, replica_groups=mesh['section'=4,'row'=2,'col'=4] {'col'}, use_global_device_ids=true, to_apply=%region_3.3.clone | all-reduce | flops 8 | bytes 64 | tf_op jit(solution)/shard_map/while
  295.2 1.2 constant_dynamic-slice_fusion.7
  296.5 21.5 %all-reduce.8.cloned.1.call-done = f32[8,3072]{1,0:T(8,128)} async-done(((f32[8,3072]{1,0:T(8,128)}), f32[8,3072]{1,0:T(8,128)}) %all-reduce.8.cloned.1.call-update) | async-done | bytes 98320 | tf_op jit(solution)/shard_map/while
  318.0 1.0 dynamic-slice_multiply_fusion.3
  320.3 10.3 %all-gather.4 = bf16[4,2,2048]{2,1,0:T(2,128)(2,1)S(1)} all-gather(bf16[1,2,2048]{2,1,0:T(2,128)(2,1)S(1)} %reshape.351), channel_id=1, replica_groups=mesh['section'=4,'row'=2,'col'=4] {'col'}, dimensions={0}, use_global_device_ids=true | all-gather | bytes 40960 | tf_op jit(solution)/shard_map/while/body/eval_jaxpr/all_gather | solution.py:89
  330.6 2.8 fusion.77
  333.4 3.4 all-gather.5
  336.8 9.8 %collective-permute-start = (bf16[8,1024]{1,0:T(8,128)(2,1)S(1)}, bf16[8,1024]{1,0:T(8,128)(2,1)S(1)}, u32[]{:S(2)}, u32[]{:S(2)}) collective-permute-start(bf16[8,1024]{1,0:T(8,128)(2,1)S(1)} %get-tuple-element.491), channel_id=1, source_target_pairs={{0,8},{8,16},{16,24},{1,9},{9,17},{17,25},{2,10},{10,18},{18,26},{... | collective-permute-start | bytes 49160 | tf_op jit(solution)/shard_map/while/body/eval_jaxpr/ppermute | solution.py:14
  348.3 4.3 fusion.65
  353.0 8.6 %all-reduce.5 = f32[8]{0:T(128)S(1)} all-reduce(f32[8]{0:T(128)S(1)} %get-tuple-element.477), channel_id=4, replica_groups=mesh['section'=4,'row'=2,'col'=4] {'col'}, use_global_device_ids=true, to_apply=%region_3.3.clone | all-reduce | flops 8 | bytes 64 | tf_op jit(solution)/shard_map/while
  362.8 1.2 constant_dynamic-slice_fusion.7
  364.1 21.5 %all-reduce.8.cloned.1.call-done = f32[8,3072]{1,0:T(8,128)} async-done(((f32[8,3072]{1,0:T(8,128)}), f32[8,3072]{1,0:T(8,128)}) %all-reduce.8.cloned.1.call-update) | async-done | bytes 98320 | tf_op jit(solution)/shard_map/while
  385.5 1.0 dynamic-slice_multiply_fusion.3
  387.8 10.3 %all-gather.4 = bf16[4,2,2048]{2,1,0:T(2,128)(2,1)S(1)} all-gather(bf16[1,2,2048]{2,1,0:T(2,128)(2,1)S(1)} %reshape.351), channel_id=1, replica_groups=mesh['section'=4,'row'=2,'col'=4] {'col'}, dimensions={0}, use_global_device_ids=true | all-gather | bytes 40960 | tf_op jit(solution)/shard_map/while/body/eval_jaxpr/all_gather | solution.py:89
  398.1 2.8 fusion.77
  400.9 3.4 all-gather.5
  404.4 9.8 %collective-permute-start = (bf16[8,1024]{1,0:T(8,128)(2,1)S(1)}, bf16[8,1024]{1,0:T(8,128)(2,1)S(1)}, u32[]{:S(2)}, u32[]{:S(2)}) collective-permute-start(bf16[8,1024]{1,0:T(8,128)(2,1)S(1)} %get-tuple-element.491), channel_id=1, source_target_pairs={{0,8},{8,16},{16,24},{1,9},{9,17},{17,25},{2,10},{10,18},{18,26},{... | collective-permute-start | bytes 49160 | tf_op jit(solution)/shard_map/while/body/eval_jaxpr/ppermute | solution.py:14
  415.8 4.3 fusion.65
  420.5 8.6 %all-reduce.5 = f32[8]{0:T(128)S(1)} all-reduce(f32[8]{0:T(128)S(1)} %get-tuple-element.477), channel_id=4, replica_groups=mesh['section'=4,'row'=2,'col'=4] {'col'}, use_global_device_ids=true, to_apply=%region_3.3.clone | all-reduce | flops 8 | bytes 64 | tf_op jit(solution)/shard_map/while
  430.3 1.2 constant_dynamic-slice_fusion.7
  431.6 21.5 %all-reduce.8.cloned.1.call-done = f32[8,3072]{1,0:T(8,128)} async-done(((f32[8,3072]{1,0:T(8,128)}), f32[8,3072]{1,0:T(8,128)}) %all-reduce.8.cloned.1.call-update) | async-done | bytes 98320 | tf_op jit(solution)/shard_map/while
  453.1 1.0 dynamic-slice_multiply_fusion.3
  455.3 10.3 %all-gather.4 = bf16[4,2,2048]{2,1,0:T(2,128)(2,1)S(1)} all-gather(bf16[1,2,2048]{2,1,0:T(2,128)(2,1)S(1)} %reshape.351), channel_id=1, replica_groups=mesh['section'=4,'row'=2,'col'=4] {'col'}, dimensions={0}, use_global_device_ids=true | all-gather | bytes 40960 | tf_op jit(solution)/shard_map/while/body/eval_jaxpr/all_gather | solution.py:89
  465.6 2.8 fusion.77
  468.4 3.4 all-gather.5
  471.9 9.8 %collective-permute-start = (bf16[8,1024]{1,0:T(8,128)(2,1)S(1)}, bf16[8,1024]{1,0:T(8,128)(2,1)S(1)}, u32[]{:S(2)}, u32[]{:S(2)}) collective-permute-start(bf16[8,1024]{1,0:T(8,128)(2,1)S(1)} %get-tuple-element.491), channel_id=1, source_target_pairs={{0,8},{8,16},{16,24},{1,9},{9,17},{17,25},{2,10},{10,18},{18,26},{... | collective-permute-start | bytes 49160 | tf_op jit(solution)/shard_map/while/body/eval_jaxpr/ppermute | solution.py:14
  (230 shorter events, 29.9 us)
Async XLA Ops:
  8.0 16.4 %copy-start.1 = (u32[32]{0:T(128)S(1)}, u32[32]{0:T(128)}, u32[]{:S(2)}) copy-start(u32[32]{0:T(128)} %get-tuple-element.547) | copy-start | bytes 388 | tf_op jit(solution)/shard_map/while
  8.0 39.9 %all-reduce.8.cloned.1.call-start = ((), (), s32[]{:S(2)}) async-start(), calls=%async_computation | async-start | bytes 196608 | tf_op jit(solution)/shard_map/while
  66.8 10.6 %collective-permute-start = (bf16[8,1024]{1,0:T(8,128)(2,1)S(1)}, bf16[8,1024]{1,0:T(8,128)(2,1)S(1)}, u32[]{:S(2)}, u32[]{:S(2)}) collective-permute-start(bf16[8,1024]{1,0:T(8,128)(2,1)S(1)} %get-tuple-element.491), channel_id=1, source_target_pairs={{0,8},{8,16},{16,24},{1,9},{9,17},{17,25},{2,10},{10,18},{18,26},{... | collective-permute-start | bytes 49160 | tf_op jit(solution)/shard_map/while/body/eval_jaxpr/ppermute | solution.py:14
  77.4 14.1 %copy-start.1 = (u32[32]{0:T(128)S(1)}, u32[32]{0:T(128)}, u32[]{:S(2)}) copy-start(u32[32]{0:T(128)} %get-tuple-element.547) | copy-start | bytes 388 | tf_op jit(solution)/shard_map/while
  77.4 38.1 %all-reduce.8.cloned.1.call-start = ((), (), s32[]{:S(2)}) async-start(), calls=%async_computation | async-start | bytes 196608 | tf_op jit(solution)/shard_map/while
  134.3 10.6 %collective-permute-start = (bf16[8,1024]{1,0:T(8,128)(2,1)S(1)}, bf16[8,1024]{1,0:T(8,128)(2,1)S(1)}, u32[]{:S(2)}, u32[]{:S(2)}) collective-permute-start(bf16[8,1024]{1,0:T(8,128)(2,1)S(1)} %get-tuple-element.491), channel_id=1, source_target_pairs={{0,8},{8,16},{16,24},{1,9},{9,17},{17,25},{2,10},{10,18},{18,26},{... | collective-permute-start | bytes 49160 | tf_op jit(solution)/shard_map/while/body/eval_jaxpr/ppermute | solution.py:14
  144.9 14.1 %copy-start.1 = (u32[32]{0:T(128)S(1)}, u32[32]{0:T(128)}, u32[]{:S(2)}) copy-start(u32[32]{0:T(128)} %get-tuple-element.547) | copy-start | bytes 388 | tf_op jit(solution)/shard_map/while
  144.9 38.1 %all-reduce.8.cloned.1.call-start = ((), (), s32[]{:S(2)}) async-start(), calls=%async_computation | async-start | bytes 196608 | tf_op jit(solution)/shard_map/while
  201.8 10.6 %collective-permute-start = (bf16[8,1024]{1,0:T(8,128)(2,1)S(1)}, bf16[8,1024]{1,0:T(8,128)(2,1)S(1)}, u32[]{:S(2)}, u32[]{:S(2)}) collective-permute-start(bf16[8,1024]{1,0:T(8,128)(2,1)S(1)} %get-tuple-element.491), channel_id=1, source_target_pairs={{0,8},{8,16},{16,24},{1,9},{9,17},{17,25},{2,10},{10,18},{18,26},{... | collective-permute-start | bytes 49160 | tf_op jit(solution)/shard_map/while/body/eval_jaxpr/ppermute | solution.py:14
  212.4 14.1 %copy-start.1 = (u32[32]{0:T(128)S(1)}, u32[32]{0:T(128)}, u32[]{:S(2)}) copy-start(u32[32]{0:T(128)} %get-tuple-element.547) | copy-start | bytes 388 | tf_op jit(solution)/shard_map/while
  212.4 38.1 %all-reduce.8.cloned.1.call-start = ((), (), s32[]{:S(2)}) async-start(), calls=%async_computation | async-start | bytes 196608 | tf_op jit(solution)/shard_map/while
  269.3 10.6 %collective-permute-start = (bf16[8,1024]{1,0:T(8,128)(2,1)S(1)}, bf16[8,1024]{1,0:T(8,128)(2,1)S(1)}, u32[]{:S(2)}, u32[]{:S(2)}) collective-permute-start(bf16[8,1024]{1,0:T(8,128)(2,1)S(1)} %get-tuple-element.491), channel_id=1, source_target_pairs={{0,8},{8,16},{16,24},{1,9},{9,17},{17,25},{2,10},{10,18},{18,26},{... | collective-permute-start | bytes 49160 | tf_op jit(solution)/shard_map/while/body/eval_jaxpr/ppermute | solution.py:14
  279.9 14.1 %copy-start.1 = (u32[32]{0:T(128)S(1)}, u32[32]{0:T(128)}, u32[]{:S(2)}) copy-start(u32[32]{0:T(128)} %get-tuple-element.547) | copy-start | bytes 388 | tf_op jit(solution)/shard_map/while
  279.9 38.1 %all-reduce.8.cloned.1.call-start = ((), (), s32[]{:S(2)}) async-start(), calls=%async_computation | async-start | bytes 196608 | tf_op jit(solution)/shard_map/while
  336.8 10.6 %collective-permute-start = (bf16[8,1024]{1,0:T(8,128)(2,1)S(1)}, bf16[8,1024]{1,0:T(8,128)(2,1)S(1)}, u32[]{:S(2)}, u32[]{:S(2)}) collective-permute-start(bf16[8,1024]{1,0:T(8,128)(2,1)S(1)} %get-tuple-element.491), channel_id=1, source_target_pairs={{0,8},{8,16},{16,24},{1,9},{9,17},{17,25},{2,10},{10,18},{18,26},{... | collective-permute-start | bytes 49160 | tf_op jit(solution)/shard_map/while/body/eval_jaxpr/ppermute | solution.py:14
  347.5 14.1 %copy-start.1 = (u32[32]{0:T(128)S(1)}, u32[32]{0:T(128)}, u32[]{:S(2)}) copy-start(u32[32]{0:T(128)} %get-tuple-element.547) | copy-start | bytes 388 | tf_op jit(solution)/shard_map/while
  347.5 38.1 %all-reduce.8.cloned.1.call-start = ((), (), s32[]{:S(2)}) async-start(), calls=%async_computation | async-start | bytes 196608 | tf_op jit(solution)/shard_map/while
  404.4 10.6 %collective-permute-start = (bf16[8,1024]{1,0:T(8,128)(2,1)S(1)}, bf16[8,1024]{1,0:T(8,128)(2,1)S(1)}, u32[]{:S(2)}, u32[]{:S(2)}) collective-permute-start(bf16[8,1024]{1,0:T(8,128)(2,1)S(1)} %get-tuple-element.491), channel_id=1, source_target_pairs={{0,8},{8,16},{16,24},{1,9},{9,17},{17,25},{2,10},{10,18},{18,26},{... | collective-permute-start | bytes 49160 | tf_op jit(solution)/shard_map/while/body/eval_jaxpr/ppermute | solution.py:14
  415.0 14.1 %copy-start.1 = (u32[32]{0:T(128)S(1)}, u32[32]{0:T(128)}, u32[]{:S(2)}) copy-start(u32[32]{0:T(128)} %get-tuple-element.547) | copy-start | bytes 388 | tf_op jit(solution)/shard_map/while
  415.0 38.1 %all-reduce.8.cloned.1.call-start = ((), (), s32[]{:S(2)}) async-start(), calls=%async_computation | async-start | bytes 196608 | tf_op jit(solution)/shard_map/while
  471.9 10.6 %collective-permute-start = (bf16[8,1024]{1,0:T(8,128)(2,1)S(1)}, bf16[8,1024]{1,0:T(8,128)(2,1)S(1)}, u32[]{:S(2)}, u32[]{:S(2)}) collective-permute-start(bf16[8,1024]{1,0:T(8,128)(2,1)S(1)} %get-tuple-element.491), channel_id=1, source_target_pairs={{0,8},{8,16},{16,24},{1,9},{9,17},{17,25},{2,10},{10,18},{18,26},{... | collective-permute-start | bytes 49160 | tf_op jit(solution)/shard_map/while/body/eval_jaxpr/ppermute | solution.py:14
  482.5 0.6 copy-start
Sparse Core Ops, SparseCore 0:
  13.5 34.4 all-reduce.7
  82.7 32.6 all-reduce.7
  150.2 32.6 all-reduce.7
  217.8 32.6 all-reduce.7
  285.3 32.6 all-reduce.7
  352.8 32.6 all-reduce.7
  420.3 32.6 all-reduce.7
